TPU v7x, 32 devices: a whole 2x2x4 slice. The times are simulated.
32 devices in a mesh: cls: 4 (over y, x), org: 8 (over z, core).
Axes of the slice: x: 2, y: 2, z: 4, core: 2. Of those that a mesh axis runs over, the one named last changes fastest.
Arguments:
- flows_start: float32 [8, 49152], P('cls', 'org'), may hold values from 150 to 300
- interaction: float32 [8, 8, 49152], P('cls', None, 'org'), may hold values from 0.2 to 2
- free_time: float32 [8, 49152], P('cls', 'org'), may hold values from 0.01 to 0.1
- capacity: float32 [49152], P('org'), may hold values from 300 to 900
- demand: int32 [8, 8, 60], P('cls', 'org'), may hold values from 0 to 15
- incidence: int32 [2, 8, 8, 2, 49152], P(None, 'cls', 'org'), may hold values from 0 to 1073741823, as said below
- step_size: float32 [2], replicated, may hold values from 0.3 to 0.6
Outputs:
- flows: float32 [8, 49152], P('cls', 'org')
- costs: float32 [8, 49152], P('cls', 'org')
- skims: float32 [2, 8, 8, 60], P(None, 'cls', 'org')
- gaps: float32 [2], replicated
Inputs may be any that keep to these rules, and one draw needn't show every extreme that they name: Bit b of incidence[k, c, o, w, l] tells whether link l lies on class c's path from anchor o to destination w * 30 + b in iteration k; each path is the union of 4 runs of 64 consecutive links (counted cyclically over the links) at drawn starts, the first of which is shared by all 30 destinations of one word.
All inputs are finite; a program needn't handle non-finite values.
Results may differ from a plain program's by a relative error of at most 0.0013.
Values sent between devices are 32-bit elements; how exact they have to be, the bound alone decides.
No kernel may reach another device: no remote copies, remote signals or barrier semaphores. Data moves between devices by JAX's collectives and lax.ppermute only.
A program may use at most 256 MiB of HBM per device.

v0:
```python
import jax
import jax.numpy as jnp
from jax import lax
from jax.sharding import PartitionSpec as P

BITS = 30
ITERS = 2


HIGH = lax.Precision.HIGHEST


def unpack_half(packed):
    shifts = jnp.arange(BITS, dtype=jnp.int32)
    bit_table = jnp.bitwise_and(jnp.right_shift(packed[..., :, None, :], shifts[:, None]), 1)
    new_shape = packed.shape[:-2] + (packed.shape[-2] * BITS, packed.shape[-1])
    return bit_table.reshape(new_shape).astype(jnp.bfloat16)


def link_cost(flows_all, inter, free, cap):
    load_sum = jnp.einsum("cel,el->cl", inter, flows_all, precision=HIGH)
    load_ratio = load_sum / cap
    square = load_ratio * load_ratio
    return free * (1.0 + 0.15 * square * square)


def split_three(values):
    upper = values.astype(jnp.bfloat16)
    remain = values - upper.astype(jnp.float32)
    middle = remain.astype(jnp.bfloat16)
    lowest = (remain - middle.astype(jnp.float32)).astype(jnp.bfloat16)
    return jnp.stack([upper, middle, lowest], axis=1)


def skim_block(bit_table, cost_block):
    parts = split_three(cost_block)
    terms = jnp.einsum("codl,cpl->cpod", bit_table, parts, preferred_element_type=jnp.float32)
    return jnp.sum(terms, axis=1)


def anchor_loads_local(packed_all, trips_half, link_shard, block_count):

    def one_block(block_index):
        word_block = lax.dynamic_slice_in_dim(packed_all, block_index * link_shard, link_shard, 3)
        bit_table = unpack_half(word_block)
        return jnp.einsum("cod,codl->cl", trips_half, bit_table, preferred_element_type=jnp.float32)

    blocks = lax.map(one_block, jnp.arange(block_count, dtype=jnp.int32))
    return jnp.moveaxis(blocks, 0, 1).reshape(blocks.shape[1], block_count * link_shard)


def make_fold(packed_all, link_shard):

    def fold_links(skim_carry, portion, first):
        turn_count = portion.shape[1] // link_shard

        def advance(skim_sum, block_index):
            offset = block_index * link_shard
            word_block = lax.dynamic_slice_in_dim(packed_all, offset, link_shard, 3)
            bit_table = unpack_half(word_block)
            cost_block = lax.dynamic_slice_in_dim(portion, offset, link_shard, 1)
            return (skim_sum + skim_block(bit_table, cost_block), None)

        result, unused = lax.scan(advance, skim_carry, jnp.arange(turn_count, dtype=jnp.int32))
        return result

    return fold_links


def both_totals(cost_part, path_part):
    return lax.psum((cost_part, path_part), ("cls", "org"))


def shards(flows_start, interaction, free_time, capacity, demand, incidence, step_size):
    org_count = lax.axis_size("org")
    link_shard = flows_start.shape[1]
    dest_count = demand.shape[2]
    class_local = demand.shape[0]
    demand_real = demand.astype(jnp.float32)
    trips_half = demand.astype(jnp.bfloat16)
    own_start = lax.axis_index("org") * link_shard
    skim_init = jnp.zeros((class_local, demand.shape[1], dest_count), jnp.float32)
    skim_list = []
    gap_list = []
    inter_full, free_full, cap_full, flow_now = (
        lax.all_gather(interaction, "org", axis=2, tiled=True),
        lax.all_gather(free_time, "org", axis=1, tiled=True),
        lax.all_gather(capacity, "org", axis=0, tiled=True),
        lax.all_gather(flows_start, "org", axis=1, tiled=True),
    )

    def full_cost(flow_value):
        flows_all = lax.all_gather(flow_value, "cls", axis=0, tiled=True)
        return link_cost(flows_all, inter_full, free_full, cap_full)

    for iteration in range(ITERS):
        cost_now = full_cost(flow_now)
        fold_links = make_fold(incidence[iteration], link_shard)
        skim_now = fold_links(skim_init, cost_now, jnp.int32(0))
        partial_value = anchor_loads_local(incidence[iteration], trips_half, link_shard, org_count)
        aon = lax.psum(partial_value, "org")
        product = lax.dynamic_slice_in_dim(cost_now * flow_now, own_start, link_shard, 1)
        cost_total, path_total = both_totals(jnp.sum(product), jnp.sum(demand_real * skim_now))
        gap_list.append((cost_total - path_total) / cost_total)
        skim_list.append(skim_now)
        flow_now = flow_now + step_size[iteration] * (aon - flow_now)
    cost_final = full_cost(flow_now)
    flow_out = lax.dynamic_slice_in_dim(flow_now, own_start, link_shard, 1)
    cost_out = lax.dynamic_slice_in_dim(cost_final, own_start, link_shard, 1)
    return (flow_out, cost_out, jnp.stack(skim_list), jnp.stack(gap_list))


def solution(mesh):
    placed = (
        P("cls", "org"),
        P("cls", None, "org"),
        P("cls", "org"),
        P("org"),
        P("cls", "org", None),
        P(None, "cls", "org", None, None),
        P(),
    )
    return jax.shard_map(
        shards,
        mesh=mesh,
        in_specs=placed,
        out_specs=(P("cls", "org"), P("cls", "org"), P(None, "cls", "org", None), P()),
        check_vma=False,
    )
```

profile of v0, /device:TPU:0, one launch (start us, length us, event | category | flops | bytes accessed | tf_op | source)
XLA Modules:
  0.0 387.4 jit_solution(10713880894416797273)
XLA Ops:
  10.9 32.3 %while.43 = (s32[]{:T(128)}, f32[8,2,6144]{2,1,0:T(2,128)S(1)}, s32[8]{0:T(128)S(1)}, s32[2,1,2,49152]{3,0,2,1:T(2,128)S(1)}, bf16[2,1,60]{2,0,1:T(2,128)(2,1)S(...) while((s32[]{:T(128)}, f32[8,2,6144]{2,1,0:T(2,128)S(1)}, s32[8]{0:T(128)S(1)}, ...), condition=%wide.region_4.5_spmd, body=%wide.region_3.4_spmd.sunk | while | flops 3686406 | bytes 3392847 | solution.py:48
  12.3 1.7 fusion.83
  16.3 1.7 fusion.83
  20.3 1.7 fusion.83
  24.4 1.7 fusion.83
  28.4 1.7 fusion.83
  32.5 1.7 fusion.83
  36.5 1.7 fusion.83
  40.5 1.7 fusion.83
  44.3 32.3 %while.42 = (s32[]{:T(128)}, f32[8,2,6144]{2,1,0:T(2,128)S(1)}, s32[8]{0:T(128)S(1)}, s32[2,1,2,49152]{3,0,2,1:T(2,128)S(1)}, bf16[2,1,60]{2,0,1:T(2,128)(2,1)S(...) while((s32[]{:T(128)}, f32[8,2,6144]{2,1,0:T(2,128)S(1)}, s32[8]{0:T(128)S(1)}, ...), condition=%wide.region_1.0_spmd, body=%wide.region_0.1_spmd.sunk | while | flops 3686406 | bytes 3392847 | solution.py:48
  77.5 17.5 %all_gather.21 = f32[2,49152]{1,0:T(2,128)} all-gather(f32[2,6144]{1,0:T(2,128)S(1)} %copy-done.7), channel_id=1, replica_groups=mesh['cls'=4,'org'=8] {'org'}, dimensions={1}, use_global_device_ids=true | all-gather | bytes 442368 | tf_op jit(solution)/shard_map/all_gather | solution.py:89
  95.7 42.7 %all-reduce.4.cloned.1.call-done = (f32[2,49152]{1,0:T(2,128)}, f32[2,49152]{1,0:T(2,128)}) async-done(((f32[2,49152]{1,0:T(2,128)}, f32[2,49152]{1,0:T(2,128)}), (f32[2,49152]{1,0:T(2,128)}, f32[2,49152]{1,0:T(2,128)})) %all-reduce.4.cloned.1.call-update) | async-done | bytes 786448 | tf_op jit(solution)/shard_map/psum | solution.py:101
  138.4 3.8 multiply_add_fusion
  143.5 15.2 %all_gather.25 = f32[49152]{0:T(1024)} all-gather(f32[6144]{0:T(1024)S(1)} %copy-done.9), channel_id=1, replica_groups=mesh['cls'=4,'org'=8] {'org'}, dimensions={0}, use_global_device_ids=true | all-gather | bytes 221184 | tf_op jit(solution)/shard_map/all_gather | solution.py:88
  158.7 14.7 %all_gather.22 = f32[2,49152]{1,0:T(2,128)S(1)} all-gather(f32[2,6144]{1,0:T(2,128)S(1)} %copy-done.8), channel_id=1, replica_groups=mesh['cls'=4,'org'=8] {'org'}, dimensions={1}, use_global_device_ids=true | all-gather | bytes 442368 | tf_op jit(solution)/shard_map/all_gather | solution.py:87
  174.8 2.5 reshape.94
  177.3 2.5 reshape.92
  179.8 24.8 %all-gather.14.cloned.1.call-done = f32[4,2,49152]{2,1,0:T(2,128)} async-done(((f32[1,2,49152]{2,1,0:T(2,128)}), f32[4,2,49152]{2,1,0:T(2,128)}) %all-gather.14.cloned.1.call-update) | async-done | bytes 1572880 | tf_op jit(solution)/shard_map/all_gather | solution.py:93
  204.6 3.6 reshape.96
  208.2 36.0 %all-gather.8.cloned.1.call-done = f32[2,8,49152]{2,1,0:T(8,128)} async-done(((f32[2,8,6144]{2,1,0:T(8,128)}), f32[2,8,49152]{2,1,0:T(8,128)}) %all-gather.8.cloned.1.call-update) | async-done | bytes 3145744 | tf_op jit(solution)/shard_map/all_gather | solution.py:86
  244.2 6.9 %multiply_reduce_fusion.1 = (f32[49152,2]{0,1:T(2,128)S(1)}, f32[49152,2]{0,1:T(2,128)S(1)}, f32[49152,2]{0,1:T(2,128)}) fusion(f32[2,8,49152]{2,1,0:T(8,128)} %all-gather.8.cloned.1.call-done, f32[49152,8]{0,1:T(8,128)S(1)} %bitcast.155, f32[49152,8]{0,1:T(8,128)} %bitcast.157, f32[49152,8]{0,1:T(8,128)S(1)} %bitcast.156), kind=kLoop, calls=%fused_computation.59 | loop fusion | flops 4423680 | bytes 9043968 | tf_op jit(solution)/shard_map/cel,el->cl/dot_general | solution.py:21
  253.4 39.4 %while.44 = (s32[]{:T(128)}, f32[2,1,60]{2,0,1:T(2,128)S(1)}, s32[8]{0:T(128)S(1)}, f32[2,49152]{1,0:T(2,128)S(1)}, s32[2,1,2,49152]{3,0,2,1:T(2,128)}, /*index=5*/s32[]{:T(128)}, s32[1]{0:T(128)}, s32[]{:T(128)}, s32[]{:T(128)}) while((s32[]{:T(128)}, f32[2,1,60]{2,0,1:T(2,128)S(1)}, s32[8]{0:T(128)S(1)}, ...), condition=%wide.region_8.9_spmd.clone, body=%wide.region_6.8_spmd.clone.sunk | while | flops 6943207 | bytes 3615725 | solution.py:64
  294.2 39.4 %while.45 = (s32[]{:T(128)}, f32[2,1,60]{2,0,1:T(2,128)S(1)}, s32[8]{0:T(128)S(1)}, f32[2,49152]{1,0:T(2,128)S(1)}, s32[2,1,2,49152]{3,0,2,1:T(2,128)}, /*index=5*/s32[]{:T(128)}, s32[1]{0:T(128)}, s32[]{:T(128)}, s32[]{:T(128)}) while((s32[]{:T(128)}, f32[2,1,60]{2,0,1:T(2,128)S(1)}, s32[8]{0:T(128)S(1)}, ...), condition=%wide.region_11.12_spmd.clone, body=%wide.region_9.11_spmd.clone.sunk | while | flops 6943207 | bytes 3615725 | solution.py:64
  334.2 39.7 %all-reduce = (f32[]{:T(128)}, f32[]{:T(128)}, f32[]{:T(128)}, f32[]{:T(128)}) all-reduce(f32[]{:T(128)} %fusion.53, f32[]{:T(128)} %get-tuple-element.186, f32[]{:T(128)} %fusion.54, f32[]{:T(128)} %get-tuple-element.185), channel_id=1, replica_groups=mesh['cls'=4,'org'=8] {'cls','org'}, use_global_device_ids=true, to_apply=%region_17.18 | all-reduce | flops 4 | bytes 32 | tf_op jit(solution)/shard_map/psum | solution.py:71
  (353 shorter events, 121.2 us)
Async XLA Ops:
  8.0 130.4 %all-reduce.4.cloned.1.call-start = ((), (), s32[]{:S(2)}) async-start(), calls=%async_computation.4 | async-start | bytes 1572864 | tf_op jit(solution)/shard_map/psum | solution.py:101
  8.0 1.5 copy-start.11
  43.2 1.0 copy-start
  43.2 1.1 copy-start.6
  43.3 34.1 %copy-start.7 = (f32[2,6144]{1,0:T(2,128)S(1)}, f32[2,6144]{1,0:T(2,128)}, u32[]{:S(2)}) copy-start(f32[2,6144]{1,0:T(2,128)} %param.15) | copy-start | bytes 147460
  76.6 0.8 copy-start.5
  76.6 65.5 %copy-start.1 = (s32[2,1,2,49152]{3,0,2,1:T(2,128)}, s32[2,1,2,49152]{3,0,2,1:T(2,128)S(1)}, u32[]{:S(2)}) copy-start(s32[2,1,2,49152]{3,0,2,1:T(2,128)S(1)} %get-tuple-element.496) | copy-start | bytes 2359300
  76.6 18.4 %copy-start.10 = (f32[2]{0:T(128)S(1)}, f32[2]{0:T(128)}, u32[]{:S(2)}) copy-start(f32[2]{0:T(128)} %param.21) | copy-start | bytes 28
  77.4 97.4 %all-gather.12.cloned.1.call-start = ((), (), s32[]{:S(2)}) async-start(), calls=%async_computation.2 | async-start | bytes 1966080 | tf_op jit(solution)/shard_map/all_gather | solution.py:93
  95.0 82.3 %all-gather.10.cloned.1.call-start = ((), (), s32[]{:S(2)}) async-start(), calls=%async_computation.1 | async-start | bytes 1966080 | tf_op jit(solution)/shard_map/all_gather | solution.py:93
  138.4 5.1 %copy-start.9 = (f32[6144]{0:T(1024)S(1)}, f32[6144]{0:T(1024)}, u32[]{:S(2)}) copy-start(f32[6144]{0:T(1024)} %param.18) | copy-start | bytes 73732
  138.4 20.3 %copy-start.8 = (f32[2,6144]{1,0:T(2,128)S(1)}, f32[2,6144]{1,0:T(2,128)}, u32[]{:S(2)}) copy-start(f32[2,6144]{1,0:T(2,128)} %param.17) | copy-start | bytes 147460
  142.2 62.4 %all-gather.14.cloned.1.call-start = ((), (), s32[]{:S(2)}) async-start(), calls=%async_computation.3 | async-start | bytes 1966080 | tf_op jit(solution)/shard_map/all_gather | solution.py:93
  142.8 101.5 %all-gather.8.cloned.1.call-start = ((), (), s32[]{:S(2)}) async-start(), calls=%async_computation | async-start | bytes 3538944 | tf_op jit(solution)/shard_map/all_gather | solution.py:86
  244.2 6.9 %copy-start.2 = (f32[49152]{0:T(1024)S(1)}, f32[49152]{0:T(1024)}, u32[]{:S(2)}) copy-start(f32[49152]{0:T(1024)} %all_gather.25) | copy-start | bytes 589828
  294.2 83.5 %copy-start.3 = (f32[49152]{0:T(1024)S(1)}, f32[49152]{0:T(1024)}, u32[]{:S(2)}) copy-start(f32[49152]{0:T(1024)} %all_gather.25) | copy-start | bytes 589828
  294.2 83.5 %copy-start.4 = (f32[49152,2]{0,1:T(2,128)S(1)}, f32[49152,2]{0,1:T(2,128)}, u32[]{:S(2)}) copy-start(f32[49152,2]{0,1:T(2,128)} %get-tuple-element.184) | copy-start | bytes 1179652
Sparse Core Ops, SparseCore 0:
  77.5 60.7 all-reduce.3
Sparse Core Ops, SparseCore 1:
  95.1 31.7 all-gather.11
  142.3 29.8 all-gather.9
  173.8 30.7 all-gather.13
  206.2 38.0 all-gather.7
where the time goes:
time: 389 us; the launch traced here: 387 us
  waiting for transfers between devices  105 us (27%)
  blocking collectives  87 us (22%)
  other arithmetic  73.1 us (19%)
  local copies, waits for them, and re-layouts  54.5 us (14%)
  matrix products  25.3 us (7%)
  loops' own time  22.7 us (6%)
  between operations  19.7 us (5%)
    convert_element_type x32, other arithmetic, unpack_half(): return bit_table.reshape(new_shape).astype(jnp.bfloat16)  55.2 us
    psum x1, waiting for transfers between devices, shards(): aon = lax.psum(partial_value, 'org')  42.7 us
    psum x1, blocking collectives, both_totals(): return lax.psum((cost_part, path_part), ('cls', 'org'))  39.7 us
    all_gather x1, waiting for transfers between devices, shards(): lax.all_gather(interaction, 'org', axis=2, tiled=True)  36 us
    all_gather x3, waiting for transfers between devices, full_cost(): flows_all = lax.all_gather(flow_value, 'cls', axis=0, tiled=True)  24.8 us
    dynamic_slice x32, local copies, waits for them, and re-layouts, fold_links(): lax.scan(advance, skim_carry, jnp.arange(turn_count, dtype=jnp.int32))  18.8 us
    all_gather x1, blocking collectives, shards(): lax.all_gather(flows_start, 'org', axis=1, tiled=True)  17.5 us
    shift_right_arithmetic x96, local copies, waits for them, and re-layouts, unpack_half(): jnp.right_shift(packed[..., :, None, :], shifts[:, None])  17.5 us
  transfers between devices with their start and end apart: 5, of which 3 were waited for; matrix products, arithmetic and copies ran while one was open for 4% of the time, Pallas kernels for 0%

commit v1 on v0

v1 whole, which is shorter than its diff:
```python
import jax
import jax.numpy as jnp
from jax import lax
from jax.experimental import pallas as pl
from jax.experimental.pallas import tpu as pltpu
from jax.sharding import PartitionSpec as P

BITS = 30
PLANES = 4
LANES = 128
ROWS = 8
UNROLL = 2


def skim_kernel(words_ref, cost_ref, out_ref):
    steps = words_ref.shape[1] // (ROWS * UNROLL)

    def advance(step, sums):
        sums = list(sums)
        for part in range(UNROLL):
            start = pl.multiple_of((step * UNROLL + part) * ROWS, ROWS)
            words = words_ref[0, pl.ds(start, ROWS), :]
            costs = cost_ref[0, pl.ds(start, ROWS), :]
            for bit in range(BITS):
                chosen = jnp.bitwise_and(words, jnp.int32(1 << bit)) != 0
                sums[bit] = sums[bit] + jnp.where(chosen, costs, 0.0)
        return tuple(sums)

    zero = jnp.zeros((ROWS, LANES), jnp.float32)
    sums = lax.fori_loop(0, steps, advance, (zero,) * BITS)
    lane = lax.broadcasted_iota(jnp.int32, (ROWS, LANES), 1)
    out = zero
    for bit in range(BITS):
        total = jnp.sum(sums[bit], axis=1, keepdims=True)
        out = jnp.where(lane == bit, total, out)
    out_ref[0] = out


def path_costs(words, costs, anchors):
    groups, rows, lanes = words.shape
    return pl.pallas_call(
        skim_kernel,
        grid=(groups,),
        in_specs=[
            pl.BlockSpec((1, rows, lanes), lambda g: (g, 0, 0)),
            pl.BlockSpec((1, rows, lanes), lambda g: (g // anchors, 0, 0)),
        ],
        out_specs=pl.BlockSpec((1, ROWS, LANES), lambda g: (g, 0, 0)),
        out_shape=jax.ShapeDtypeStruct((groups, ROWS, LANES), jnp.float32),
        name="path_costs",
    )(words, costs)


def link_cost(flows_all, inter, free, cap):
    load_sum = jnp.sum(inter * flows_all[None], axis=1)
    load_ratio = load_sum / cap
    square = load_ratio * load_ratio
    return free * (1.0 + 0.15 * square * square)


def own_loads(demand, incidence):
    classes, anchors, dests = demand.shape
    by_word = demand.reshape(classes, anchors, dests // BITS, BITS)
    shifts = jnp.arange(BITS, dtype=jnp.int32)
    total = 0
    for plane in range(PLANES):
        bits = jnp.bitwise_and(jnp.right_shift(by_word, plane), 1)
        mask = jnp.sum(jnp.left_shift(bits, shifts), axis=-1)
        count = lax.population_count(jnp.bitwise_and(incidence, mask[None, ..., None]))
        total = total + jnp.left_shift(count, plane)
    return jnp.sum(total, axis=(2, 3)).astype(jnp.float32)


def shards(flows_start, interaction, free_time, capacity, demand, incidence, step_size):
    orgs = lax.axis_size("org")
    iters, classes, anchors, dwords, links = incidence.shape
    own = flows_start.shape[1]
    blocks = links // LANES

    partial = own_loads(demand, incidence)
    spread = jnp.moveaxis(partial.reshape(iters, classes, orgs, own), 2, 0)
    received = lax.all_to_all(spread, "org", 0, 0)
    aon = jnp.sum(received, axis=0)

    state = jnp.concatenate([flows_start[None], aon], axis=0)
    state_all = lax.all_gather(state, "cls", axis=1, tiled=True)
    flow_all = state_all[0]
    flow_own = flows_start
    cost_list = []
    totals = []
    for k in range(iters):
        cost = link_cost(flow_all, interaction, free_time, capacity)
        cost_list.append(cost)
        totals.append(jnp.sum(cost * flow_own))
        totals.append(jnp.sum(cost * aon[k]))
        flow_all = flow_all + step_size[k] * (state_all[k + 1] - flow_all)
        flow_own = flow_own + step_size[k] * (aon[k] - flow_own)
    cost_final = link_cost(flow_all, interaction, free_time, capacity)

    costs = jnp.stack(cost_list)
    costs_all = lax.all_gather(costs, "org", axis=2, tiled=True)
    sums = lax.psum(jnp.stack(totals), ("cls", "org")).reshape(iters, 2)
    gaps = (sums[:, 0] - sums[:, 1]) / sums[:, 0]

    groups = iters * classes * anchors
    words = incidence.reshape(iters, classes, anchors, dwords, blocks, LANES)
    words = jnp.swapaxes(words, 3, 4).reshape(groups, blocks * dwords, LANES)
    wide = costs_all.reshape(iters * classes, blocks, 1, LANES)
    wide = jnp.broadcast_to(wide, (iters * classes, blocks, dwords, LANES))
    wide = wide.reshape(iters * classes, blocks * dwords, LANES)
    found = path_costs(words, wide, anchors)
    found = found.reshape(groups, ROWS // dwords, dwords, LANES).sum(1)
    skims = found[:, :, :BITS].reshape(iters, classes, anchors, dwords * BITS)
    return (flow_own, cost_final, skims, gaps)


def solution(mesh):
    placed = (
        P("cls", "org"),
        P("cls", None, "org"),
        P("cls", "org"),
        P("org"),
        P("cls", "org", None),
        P(None, "cls", "org", None, None),
        P(),
    )
    return jax.shard_map(
        shards,
        mesh=mesh,
        in_specs=placed,
        out_specs=(P("cls", "org"), P("cls", "org"), P(None, "cls", "org", None), P()),
        check_vma=False,
    )
```

time: 389 us -> 127 us (0.33)
  waiting for transfers between devices: 105 us -> 20.4 us
  other arithmetic: 73.1 us -> 16.9 us
  local copies, waits for them, and re-layouts: 54.5 us -> 6.69 us
  matrix products: 25.3 us -> 0 us
  loops' own time: 22.7 us -> 0 us
  blocking collectives: 87 us -> 64.7 us
  between operations: 19.7 us -> 0.78 us
  Pallas kernels: 0 us -> 10.1 us
  starting transfers between devices: 0.21 us -> 6.49 us
    all_gather x4 -> x0, waiting for transfers between devices: 60.8 us -> none  [the longest x1 36 us: shards(): lax.all_gather(interaction, 'org', axis=2, tiled=True)]
    convert_element_type x33 -> x1, other arithmetic: 55.2 us -> 0.27 us  [own_loads(): return jnp.sum(total, axis=(2, 3)).astype(jnp.float32)]
    psum x1 -> x0, waiting for transfers between devices: 42.7 us -> none  [shards(): aon = lax.psum(partial_value, 'org')]
    dot_general x32 -> x0, matrix products: 25.3 us -> none  [the longest x16 14.3 us: one_block(): jnp.einsum('cod,codl->cl', trips_half, bit_table, preferred_element_type=...]
    another operation x4 -> x0, loops' own time: 22.7 us -> none  [the longest x2 11.6 us: fold_links(): lax.scan(advance, skim_carry, jnp.arange(turn_count, dtype=jnp.int32))]
    all_to_all x0 -> x1, waiting for transfers between devices: none -> 20.4 us  [shards(): received = lax.all_to_all(spread, 'org', 0, 0)]
    dynamic_slice x33 -> x0, local copies, waits for them, and re-layouts: 20.2 us -> none  [the longest x32 18.8 us: fold_links(): lax.scan(advance, skim_carry, jnp.arange(turn_count, dtype=jnp.int32))]
    all_gather x3 -> x2, blocking collectives: 47.3 us -> 27.4 us  [the longest x1 16.1 us: shards(): costs_all = lax.all_gather(costs, 'org', axis=2, tiled=True)]
  transfers between devices with their start and end apart: 5 -> 1, of which waited for: 3 -> 1; matrix products, arithmetic and copies ran while one was open for 4% -> 0% of each run, Pallas kernels for 0% -> 0%
where the time goes in v1:
time: 127 us; the launch traced here: 126 us
  blocking collectives  64.7 us (51%)
  waiting for transfers between devices  20.4 us (16%)
  other arithmetic  16.9 us (13%)
  Pallas kernels  10.1 us (8%)
  local copies, waits for them, and re-layouts  6.69 us (5%)
  starting transfers between devices  6.49 us (5%)
    psum x1, blocking collectives, shards(): sums = lax.psum(jnp.stack(totals), ('cls', 'org')).reshape(iters, 2)  37.3 us
    all_to_all x1, waiting for transfers between devices, shards(): received = lax.all_to_all(spread, 'org', 0, 0)  20.4 us
    all_gather x1, blocking collectives, shards(): costs_all = lax.all_gather(costs, 'org', axis=2, tiled=True)  16.1 us
    all_gather x1, blocking collectives, shards(): state_all = lax.all_gather(state, 'cls', axis=1, tiled=True)  11.3 us
    pallas_call x1, Pallas kernels, path_costs(): pl.pallas_call(skim_kernel, grid=(groups,), in_specs=[pl.BlockSpec((1, ro...  10.1 us
    all_to_all x1, starting transfers between devices, shards(): received = lax.all_to_all(spread, 'org', 0, 0)  6.49 us
    reduce_sum x1, other arithmetic, own_loads(): return jnp.sum(total, axis=(2, 3)).astype(jnp.float32)  6.22 us
    reduce_sum x1, other arithmetic, shards(): totals.append(jnp.sum(cost * flow_own))  2.84 us
  transfers between devices with their start and end apart: 1, of which 1 were waited for; matrix products, arithmetic and copies ran while one was open for 0% of the time, Pallas kernels for 0%

profile of v1, /device:TPU:0, one launch (start us, length us, event | category | flops | bytes accessed | tf_op | source)
XLA Modules:
  0.0 126.0 jit_solution(4686243225729851521)
XLA Ops:
  0.6 0.7 and_reduce_fusion.3
  1.8 0.2 shift-left_reduce_fusion
  2.0 6.2 %add_reduce_fusion = s32[2,2,49152]{2,1,0:T(2,128)S(1)} fusion(s32[2,2,1,2,49152]{4,3,2,1,0:T(2,128)} %param.12, s32[2,2]{1,0:T(2,128)S(1)} %get-tuple-element.26, s32[2,2]{1,0:T(2,128)S(1)} %get-tuple-element.27, s32[2,2]{1,0:T(2,128)S(1)} %get-tuple-element.28, s32[2,2]{1,0:T(2,128)S(1)} %get-tuple-element.29), kind=kLoop, calls=%fused_computation | loop fusion | flops 6094848 | bytes 2359360 | tf_op jit(solution)/shard_map/reduce_sum | solution.py:71
  8.2 0.3 convert_element_type.7
  8.5 0.7 convert_element_type.8
  9.2 1.5 %copy.18 = f32[8,2,2,6144]{3,2,1,0:T(2,128)} copy(f32[8,2,2,6144]{3,0,2,1:T(8,128)S(1)} %bitcast.45) | data formatting | bytes 1572864 | tf_op jit(solution)/shard_map/transpose | solution.py:81
  10.6 6.5 %all-to-all-start = ((f32[8,2,2,6144]{3,2,1,0:T(2,128)}), f32[8,2,2,6144]{3,2,1,0:T(2,128)S(1)}, u32[]{:S(2)}, u32[]{:S(2)}) async-start(f32[8,2,2,6144]{3,2,1,0:T(2,128)} %copy.18), calls=%async_computation | async-start | bytes 1572864 | tf_op jit(solution)/shard_map/all_to_all | solution.py:82
  17.1 0.6 fusion.13
  17.7 20.4 %all-to-all-done = f32[8,2,2,6144]{3,2,1,0:T(2,128)S(1)} async-done(((f32[8,2,2,6144]{3,2,1,0:T(2,128)}), f32[8,2,2,6144]{3,2,1,0:T(2,128)S(1)}, u32[]{:S(2)}, u32[]{:S(2)}) %all-to-all-start) | async-done | bytes 786464 | tf_op jit(solution)/shard_map/all_to_all | solution.py:82
  38.1 0.3 reduce_sum.131
  38.6 11.3 %all_gather.6 = f32[3,8,6144]{2,0,1:T(4,128)S(1)} all-gather(f32[3,2,6144]{2,0,1:T(4,128)S(1)} %copy.19), channel_id=1, replica_groups=mesh['cls'=4,'org'=8] {'cls'}, dimensions={1}, use_global_device_ids=true | all-gather | bytes 737280 | tf_op jit(solution)/shard_map/all_gather | solution.py:86
  49.9 1.9 %fusion.1 = (f32[1,8,6144]{2,0,1:T(1,128)S(1)}, f32[1,8,6144]{2,0,1:T(1,128)S(1)}, f32[1,8,6144]{2,0,1:T(1,128)S(1)}) fusion(f32[3,8,6144]{2,0,1:T(4,128)S(1)} %all_gather.6, f32[]{:T(128)} %bitcast.3, f32[]{:T(128)} %bitcast), kind=kLoop, calls=%fused_computation.6 | loop fusion | flops 294912 | bytes 1179656 | tf_op jit(solution)/shard_map/add | solution.py:96
  52.0 0.5 multiply_reduce_fusion.1
  52.5 2.8 %multiply_reduce_fusion.4 = (f32[]{:T(128)}, f32[]{:T(128)}, f32[]{:T(128)}, f32[]{:T(128)}, f32[2,6144]{1,0:T(2,128)S(1)}, /*index=5*/f32[2,6144]{1,0:T(2,128)S(1)}, f32[2,6144]{1,0:T(2,128)}, f32[2,6144]{1,0:T(2,128)}) fusion(f32[2,6144]{1,0:T(2,128)S(1)} %copy-done.1, f32[2,2,6144]{2,1,0:T(2,128)S(1)} %reduce_sum.131, f32[]{:T(128)} %bitcast, ...), kind=kLoop, calls=%fused_computation.30 | loop fusion | flops 393212 | bytes 565272 | tf_op jit(solution)/shard_map/reduce_sum | solution.py:94
  55.3 2.6 %pad_maximum_fusion.2 = f32[4]{0:T(128)S(1)} fusion(f32[1]{0:T(128)} %bitcast.16, f32[1]{0:T(128)} %bitcast.15, f32[1]{0:T(128)} %bitcast.14, f32[1]{0:T(128)} %bitcast.13), kind=kLoop, calls=%fused_computation.46 | loop fusion | flops 12 | bytes 32 | tf_op jit(solution)/shard_map/stack | solution.py:102
  58.0 37.3 %psum.7 = f32[2,2]{1,0:T(2,128)S(1)} all-reduce(f32[2,2]{1,0:T(2,128)S(1)} %reshape.180), channel_id=1, replica_groups=mesh['cls'=4,'org'=8] {'cls','org'}, use_global_device_ids=true, to_apply=%region_14.0 | all-reduce | flops 4 | bytes 32 | tf_op jit(solution)/shard_map/psum | solution.py:102
  95.3 0.2 slice_reduce_fusion
  95.5 16.1 %all_gather.7 = f32[2,2,49152]{2,1,0:T(2,128)S(1)} all-gather(f32[2,2,6144]{2,1,0:T(2,128)S(1)} %pad_maximum_fusion.1), channel_id=1, replica_groups=mesh['cls'=4,'org'=8] {'org'}, dimensions={2}, use_global_device_ids=true | all-gather | bytes 884736 | tf_op jit(solution)/shard_map/all_gather | solution.py:101
  111.7 0.7 broadcast_in_dim.7
  112.3 1.7 %broadcast_in_dim.8 = f32[4,384,2,128]{3,2,1,0:T(2,128)} broadcast(f32[4,384,128]{2,1,0:T(8,128)S(1)} %broadcast_in_dim.7), dimensions={0,1,3} | broadcast | bytes 2359296 | tf_op jit(solution)/shard_map/broadcast_in_dim | solution.py:109
  114.0 10.1 %path_costs.1 = f32[4,8,128]{2,1,0:T(8,128)} custom-call(s32[4,768,128]{2,1,0:T(8,128)} %bitcast.43, f32[4,768,128]{2,1,0:T(8,128)} %bitcast.44), custom_call_target="tpu_custom_call" | custom-call | tf_op jit(solution)/shard_map/path_costs/pallas_call | solution.py:41
  124.1 0.7 reduce_sum.135
  124.8 0.7 reshape.179
  125.5 0.5 subtract_divide_fusion
  (22 shorter events, 1.0 us)
Async XLA Ops:
  9.1 8.0 %copy-start.4 = (f32[2]{0:T(128)S(1)}, f32[2]{0:T(128)}, u32[]{:S(2)}) copy-start(f32[2]{0:T(128)} %param.13) | copy-start | bytes 28
  10.6 27.8 %copy-start.1 = (f32[2,6144]{1,0:T(2,128)S(1)}, f32[2,6144]{1,0:T(2,128)}, u32[]{:S(2)}) copy-start(f32[2,6144]{1,0:T(2,128)} %param.7) | copy-start | bytes 147460
  10.6 27.4 %all-to-all-start = ((f32[8,2,2,6144]{3,2,1,0:T(2,128)}), f32[8,2,2,6144]{3,2,1,0:T(2,128)S(1)}, u32[]{:S(2)}, u32[]{:S(2)}) async-start(f32[8,2,2,6144]{3,2,1,0:T(2,128)} %copy.18), calls=%async_computation | async-start | bytes 1572864 | tf_op jit(solution)/shard_map/all_to_all | solution.py:82
  38.6 13.4 %copy-start = (f32[2,8,6144]{2,1,0:T(8,128)S(1)}, f32[2,8,6144]{2,1,0:T(8,128)}, u32[]{:S(2)}) copy-start(f32[2,8,6144]{2,1,0:T(8,128)} %param.8) | copy-start | bytes 1179652
  49.9 2.6 %copy-start.2 = (f32[2,6144]{1,0:T(2,128)S(1)}, f32[2,6144]{1,0:T(2,128)}, u32[]{:S(2)}) copy-start(f32[2,6144]{1,0:T(2,128)} %param.9) | copy-start | bytes 147460
  49.9 2.6 %copy-start.3 = (f32[6144]{0:T(1024)S(1)}, f32[6144]{0:T(1024)}, u32[]{:S(2)}) copy-start(f32[6144]{0:T(1024)} %param.10) | copy-start | bytes 73732
